TPU v7x, 256 devices: a whole 4x4x8 slice. The times are simulated.
256 devices in a mesh: seq: 32 (over y, z), head: 8 (over x, core).
Axes of the slice: x: 4, y: 4, z: 8, core: 2. Of those that a mesh axis runs over, the one named last changes fastest.
Arguments:
- head_inputs: bfloat16 [65536, 5120], P('seq', 'head'), may hold values from -6 to 6
- gate_inputs: bfloat16 [65536, 5120], P('seq', 'head'), may hold values from -6 to 6
- step_raw: bfloat16 [65536, 80], P('seq', 'head'), may hold values from -9 to 2048
- decay_log: float32 [80], replicated, may hold values from -12 to 0
- state_write: bfloat16 [65536, 128], P(('seq', 'head')), may hold values from -6 to 6
- state_read: bfloat16 [65536, 128], P(('seq', 'head')), may hold values from -0.5 to 0.5
- skip_gain: float32 [80], replicated, may hold values from 0.5 to 2
- norm_gain: float32 [5120], replicated, may hold values from 0.1 to 1.9
Outputs:
- scan_output: bfloat16 [65536, 5120], P('seq', 'head')
All inputs are finite; a program needn't handle non-finite values.
Results may differ from a plain program's by a relative error of at most 0.005.
Values may be sent and summed in bfloat16 or wider, within the bound.
A program may use at most 128 MiB of HBM per device.

v0:
```python
import math

import jax
import jax.numpy as jnp
from jax import lax
from jax.sharding import Mesh
from jax.sharding import PartitionSpec as P

HEADS = 80
HEAD_DIM = 64
SPAN = 256
SEQ = ("seq_0", "seq_1")
SEQ_HEAD = ("seq_0", "seq_1", "head")


def side_by_side(arrays, axis, dim, along):
    widths = [a.shape[along] for a in arrays]
    both = jnp.concatenate(arrays, axis=along)
    filled = lax.all_gather(both, axis, axis=dim, tiled=True)
    return tuple(jnp.split(filled, [sum(widths[:k]) for k in range(1, len(widths))], axis=along))


def filled_with(value, identity):
    return jax.tree.map(
        lambda part, zero: jnp.zeros_like(part) + jnp.asarray(zero, part.dtype), value, identity
    )


def carried_in(value, axes, combine, identity):
    before = start = filled_with(value, identity)
    subtotal = value
    for axis in reversed(axes):
        devices, here = (lax.axis_size(axis), lax.axis_index(axis))
        pieces = jax.tree.map(lambda part: lax.all_gather(part, axis), subtotal)
        inside, subtotal = (start, start)
        for k in range(devices):
            passed = k < here
            subtotal = combine(subtotal, jax.tree.map(lambda part: part[k], pieces))
            inside = jax.tree.map(lambda new, old: jnp.where(passed, new, old), subtotal, inside)
        before = combine(inside, before)
    return before


def from_everyone(value, axis):
    devices = lax.axis_size(axis)
    return lax.all_to_all(
        jnp.broadcast_to(value[None], (devices, *value.shape)), axis, 0, 0, tiled=True
    )


def of_everyone(value, axis):
    everything = from_everyone(value, axis)
    return jnp.sum(everything, axis=0)


def combine(earlier, later):
    return (earlier[0] + later[0], jnp.exp(later[0])[:, None, None] * earlier[1] + later[1])


def intra_block(values, running, step_size, scores):
    length = running.shape[1]
    row_index = lax.broadcasted_iota(jnp.int32, (length, length), 0)
    col_index = lax.broadcasted_iota(jnp.int32, (length, length), 1)
    lower = col_index <= row_index
    by_head = jnp.moveaxis(running, 2, 1)
    weight_step = jnp.moveaxis(step_size, 2, 1)
    spread = by_head[:, :, :, None] - by_head[:, :, None, :]
    mixing = (
        jnp.where(lower, jnp.exp(jnp.where(lower, spread, 0.0)), 0.0)
        * scores[:, None]
        * weight_step[:, :, None, :]
    )
    mixing = mixing.astype(jnp.bfloat16)
    return jnp.einsum("khtu,kuhp->kthp", mixing, values, preferred_element_type=jnp.float32)


def block_pieces(values, step_raw, writes, reads, decay_rate, skip_gain):
    tokens = values.shape[0]
    heads = decay_rate.shape[0]
    width = values.shape[1] // heads
    blocks = tokens // SPAN
    group = math.gcd(heads, 4)
    groups = heads // group
    step_size = jax.nn.softplus(step_raw.astype(jnp.float32)).reshape(blocks, SPAN, heads)
    running = jnp.cumsum(-decay_rate * step_size, axis=1)
    shaped = values.reshape(blocks, SPAN, heads, width)
    write_blocks = writes.reshape(blocks, SPAN, -1)
    read_blocks = reads.reshape(blocks, SPAN, -1)
    scores = jnp.einsum(
        "ktn,kun->ktu", read_blocks, write_blocks, preferred_element_type=jnp.float32
    )

    def per_group(item):
        return intra_block(item[0], item[1], item[2], scores)

    split_values = jnp.moveaxis(shaped.reshape(blocks, SPAN, groups, group, width), 2, 0)
    split_running = jnp.moveaxis(running.reshape(blocks, SPAN, groups, group), 2, 0)
    split_step = jnp.moveaxis(step_size.reshape(blocks, SPAN, groups, group), 2, 0)
    mixed_groups = lax.map(per_group, (split_values, split_running, split_step))
    local = jnp.moveaxis(mixed_groups, 0, 2).reshape(blocks, SPAN, heads, width)
    local = local + skip_gain[:, None] * shaped.astype(jnp.float32)
    tail = jnp.exp(running[:, -1:, :] - running) * step_size
    weighted = (shaped * tail[..., None]).astype(jnp.bfloat16)
    states = jnp.einsum(
        "kuhp,kun->khpn", weighted, write_blocks, preferred_element_type=jnp.float32
    )
    return (local, running, states, running[:, -1, :], read_blocks)


def within_device(totals, states):

    def advance(carry, item):
        return (combine(carry, item), carry)

    start = (jnp.zeros_like(totals[0]), jnp.zeros_like(states[0]))
    return lax.scan(advance, start, (totals, states))


def finish_blocks(local, running, read_blocks, before, earlier_state):
    entering = (jnp.exp(before[0])[:, :, None, None] * earlier_state[None] + before[1]).astype(
        jnp.bfloat16
    )
    inter = jnp.einsum("ktn,khpn->kthp", read_blocks, entering, preferred_element_type=jnp.float32)
    ssm = local + jnp.exp(running)[..., None] * inter
    return ssm.reshape(ssm.shape[0] * ssm.shape[1], -1)


def on_device(
    head_inputs, gate_inputs, step_raw, decay_log, state_write, state_read, skip_gain, norm_gain
):
    heads = head_inputs.shape[1] // HEAD_DIM
    first = lax.axis_index("head") * heads
    decay_rate = jnp.exp(lax.dynamic_slice_in_dim(decay_log, first, heads))
    skips = lax.dynamic_slice_in_dim(skip_gain, first, heads)
    gains = lax.dynamic_slice_in_dim(norm_gain, first * HEAD_DIM, heads * HEAD_DIM)
    writes, reads = side_by_side((state_write, state_read), "head", 0, 1)
    local, running, states, totals, read_blocks = block_pieces(
        head_inputs, step_raw, writes, reads, decay_rate, skips
    )
    last, before = within_device(totals, states)
    identity = (jnp.zeros_like(last[0]), jnp.zeros_like(last[1]))
    coming = carried_in(last, SEQ, combine, identity)
    earlier_state = coming[1]
    ssm = finish_blocks(local, running, read_blocks, before, earlier_state)
    gated = ssm * jax.nn.silu(gate_inputs.astype(jnp.float32))
    squares = of_everyone(jnp.sum(gated * gated, axis=1), "head")
    factor = lax.rsqrt(squares[:, None] / (HEADS * HEAD_DIM) + 1e-05)
    return (gated * factor * gains).astype(jnp.bfloat16)


def solution(mesh):
    finer = Mesh(mesh.devices.reshape(4, 8, mesh.shape["head"]), ("seq_0", "seq_1", "head"))
    placed = (
        P(SEQ, "head"),
        P(SEQ, "head"),
        P(SEQ, "head"),
        P(),
        P(SEQ_HEAD, None),
        P(SEQ_HEAD, None),
        P(),
        P(),
    )
    return jax.shard_map(
        on_device, mesh=finer, in_specs=placed, out_specs=P(SEQ, "head"), check_vma=False
    )
```

profile of v0, /device:TPU:1, one launch (start us, length us, event | category | flops | bytes accessed | tf_op | source)
XLA Modules:
  0.0 209.0 jit_solution(3136412470189299279)
XLA Ops:
  6.5 1.7 pad_maximum_fusion
  8.3 0.9 compare_select_fusion
  10.2 4.6 %reduce-window.6 = f32[8,10,2,128]{3,1,2,0:T(8,128)S(1)} reduce-window(f32[8,10,2,128]{3,1,2,0:T(8,128)S(1)} %copy.69, f32[]{:T(128)} %constant.34.clone.1), window={size=1x1x1x128 pad=0_0x0_0x0_0x127_0}, to_apply=%region_0.1 | reduce-window | flops 2600960 | bytes 163844 | tf_op jit(solution)/shard_map/reduce-window
  16.9 3.5 %copy.77 = f32[2048,640]{0,1:T(8,128)} copy(bf16[2048,640]{1,0:T(8,128)(2,1)S(1)} %copy-done.3) | data formatting | bytes 7864320 | tf_op jit(solution)/shard_map/convert_element_type | solution.py:101
  20.4 5.0 %copy.97 = f32[80,8,8,256]{3,2,1,0:T(8,128)S(1)} copy(f32[80,8,8,256]{3,1,2,0:T(8,128)} %bitcast.207) | data formatting | bytes 10485760
  25.5 2.2 %copy-done = f32[80,8,8,256]{3,2,1,0:T(8,128)} copy-done((f32[80,8,8,256]{3,2,1,0:T(8,128)}, f32[80,8,8,256]{3,2,1,0:T(8,128)S(1)}, u32[]{:S(2)}) %copy-start) | copy-done | bytes 5242904
  28.3 10.9 %all-gather.7.cloned.1.call-done = bf16[2048,256]{1,0:T(8,128)(2,1)} async-done(((bf16[256,256]{1,0:T(8,128)(2,1)}), bf16[2048,256]{1,0:T(8,128)(2,1)}) %all-gather.7.cloned.1.call-update) | async-done | bytes 1048592 | tf_op jit(solution)/shard_map/all_gather | solution.py:19
  39.2 1.3 fusion.53
  40.5 2.3 %fusion.20 = f32[8,10,64,128]{3,2,1,0:T(8,128)} fusion(bf16[8,256,128,1]{2,1,3,0:T(8,128)(2,1)S(1)} %bitcast.214, bf16[8,256,10,64]{1,0,3,2:T(8,128)(2,1)S(1)} %multiply_convert_fusion.7), kind=kOutput, calls=%fused_computation.38 | convolution fusion | flops 335544320 | bytes 5767168 | tf_op jit(solution)/shard_map/kuhp,kun->khpn/dot_general | solution.py:104
  42.8 35.0 %while.28 = (s32[]{:T(128)}, f32[10]{0:T(128)}, f32[10,64,128]{2,1,0:T(8,128)S(1)}, f32[8,10]{1,0:T(8,128)}, f32[8,10,64,128]{3,2,1,0:T(8,128)}, /*index=5*/f32[...) while((s32[]{:T(128)}, f32[10]{0:T(128)}, f32[10,64,128]{2,1,0:T(8,128)S(1)}, ...), condition=%wide.region_5.6_spmd.clone, body=%wide.region_4.5_spmd.clone.sunk | while | flops 327703 | bytes 1638849 | solution.py:116
  42.8 1.3 fusion.62
  44.8 1.1 bitcast_add_fusion.2
  45.9 1.3 dynamic_update_slice.21
  47.2 1.3 fusion.62
  49.2 1.1 bitcast_add_fusion.2
  50.2 1.3 dynamic_update_slice.21
  51.5 1.3 fusion.62
  53.6 1.1 bitcast_add_fusion.2
  54.6 1.3 dynamic_update_slice.21
  55.9 1.3 fusion.62
  57.9 1.1 bitcast_add_fusion.2
  59.0 1.3 dynamic_update_slice.21
  60.3 1.3 fusion.62
  62.3 1.1 bitcast_add_fusion.2
  63.4 1.3 dynamic_update_slice.21
  64.7 1.3 fusion.62
  66.7 1.1 bitcast_add_fusion.2
  67.8 1.3 dynamic_update_slice.21
  69.1 1.3 fusion.62
  71.1 1.1 bitcast_add_fusion.2
  72.1 1.3 dynamic_update_slice.21
  73.4 1.3 fusion.62
  75.4 1.1 bitcast_add_fusion.2
  76.5 1.3 dynamic_update_slice.21
  78.6 3.0 %copy.68 = bf16[2048,640]{0,1:T(8,128)(2,1)S(1)} copy(bf16[2048,640]{1,0:T(8,128)(2,1)} %param.12) | data formatting | bytes 5242880 | tf_op args[0]
  81.7 2.4 %copy.94 = bf16[80,8,8,256]{3,2,1,0:T(8,128)(2,1)} copy(bf16[80,8,8,256]{3,1,2,0:T(8,128)(2,1)S(1)} %bitcast.209) | data formatting | bytes 5242880
  85.4 3.0 %copy.84 = bf16[2048,640]{0,1:T(8,128)(2,1)S(1)} copy(bf16[2048,640]{1,0:T(8,128)(2,1)} %param.13) | data formatting | bytes 5242880 | tf_op args[1]
  89.9 14.9 %all-reduce = f32[80]{0:T(128)S(1)} all-reduce(f32[80]{0:T(128)S(1)} %dynamic-update-slice), channel_id=2, replica_groups=mesh['seq_0'=4,'seq_1'=8,'head'=8] {'seq_1'}, use_global_device_ids=true, to_apply=%add | all-reduce | flops 80 | bytes 640
  106.2 2.8 %fusion.54 = f32[8,256,256]{2,1,0:T(8,128)} fusion(bf16[8,256,128]{2,1,0:T(8,128)(2,1)S(1)} %bitcast.212, bf16[8,256,128]{2,1,0:T(8,128)(2,1)} %bitcast.215), kind=kOutput, calls=%fused_computation.121 | convolution fusion | flops 134217728 | bytes 3145728 | tf_op jit(solution)/shard_map/ktn,kun->ktu/dot_general | solution.py:89
  109.1 8.6 %all-gather.11.cloned.1.call-done = f32[80,64,128]{2,1,0:T(8,128)} async-done(((f32[10,64,128]{2,1,0:T(8,128)}), f32[80,64,128]{2,1,0:T(8,128)}) %all-gather.11.cloned.1.call-update) | async-done | bytes 2621456 | tf_op jit(solution)/shard_map/all_gather | solution.py:34
  117.7 2.7 %fusion.28 = (f32[1,10,64,128]{3,2,1,0:T(8,128)}, f32[1,10,64,128]{3,2,1,0:T(8,128)}) fusion(f32[80,64,128]{2,1,0:T(8,128)} %all-gather.11.cloned.1.call-done, f32[10]{0:T(128)S(1)} %get-tuple-element.180, f32[10]{0:T(128)S(1)} %get-tuple-element.181, f32[10]{0:T(128)S(1)} %get-tuple-element.175, f32[10]{0:T(128)S(1)} %get-tuple-element.174, ...), kind=kLoop, calls=%fused_computation.53 | loop fusion | flops 1228800 | bytes 3277120 | tf_op jit(solution)/shard_map/add | solution.py:57
  120.5 24.4 %while.27 = (s32[]{:T(128)}, f32[5,8,256,2,64]{2,4,3,1,0:T(8,128)}, bf16[5,8,256,2,64]{2,1,4,3,0:T(8,128)(2,1)}, f32[5,8,256,2]{2,1,3,0:T(8,128)S(1)}, f32[8,256...) while((s32[]{:T(128)}, f32[5,8,256,2,64]{2,4,3,1,0:T(8,128)}, ...), condition=%wide.region_3.4_spmd, body=%wide.region_2.3_spmd.sunk | while | flops 140574720 | bytes 5029985 | solution.py:99
  120.6 1.1 constant_dynamic-slice_fusion.7
  121.7 3.7 %fusion.61 = f32[5,8,256,2,64]{2,4,3,1,0:T(8,128)} fusion(f32[5,8,256,2,64]{2,4,3,1,0:T(8,128)} %get-tuple-element.280, s32[]{:T(128)S(6)} %copy.124, f32[8,2,256]{2,1,0:T(2,128)S(1)} %bitcast.222, f32[8,256,256]{2,1,0:T(8,128)} %get-tuple-element.290, f32[8,2,256]{2,1,0:T(2,128)S(1)} %bitcast.223, pred[256,256]{1,0:T(8,128)(4,1)S(1)} %iota_compare_fusion.2, ...), kind=kOutput, calls=%fused_computation.9.clone.1 | convolution fusion | flops 140509184 | bytes 3784708 | tf_op jit(solution)/shard_map/while/body/eval_jaxpr/khtu,kuhp->kthp/dot_general | solution.py:74
  125.5 1.1 constant_dynamic-slice_fusion.7
  126.6 3.7 %fusion.61 = f32[5,8,256,2,64]{2,4,3,1,0:T(8,128)} fusion(f32[5,8,256,2,64]{2,4,3,1,0:T(8,128)} %get-tuple-element.280, s32[]{:T(128)S(6)} %copy.124, f32[8,2,256]{2,1,0:T(2,128)S(1)} %bitcast.222, f32[8,256,256]{2,1,0:T(8,128)} %get-tuple-element.290, f32[8,2,256]{2,1,0:T(2,128)S(1)} %bitcast.223, pred[256,256]{1,0:T(8,128)(4,1)S(1)} %iota_compare_fusion.2, ...), kind=kOutput, calls=%fused_computation.9.clone.1 | convolution fusion | flops 140509184 | bytes 3784708 | tf_op jit(solution)/shard_map/while/body/eval_jaxpr/khtu,kuhp->kthp/dot_general | solution.py:74
  130.3 1.1 constant_dynamic-slice_fusion.7
  131.4 3.8 %fusion.61 = f32[5,8,256,2,64]{2,4,3,1,0:T(8,128)} fusion(f32[5,8,256,2,64]{2,4,3,1,0:T(8,128)} %get-tuple-element.280, s32[]{:T(128)S(6)} %copy.124, f32[8,2,256]{2,1,0:T(2,128)S(1)} %bitcast.222, f32[8,256,256]{2,1,0:T(8,128)} %get-tuple-element.290, f32[8,2,256]{2,1,0:T(2,128)S(1)} %bitcast.223, pred[256,256]{1,0:T(8,128)(4,1)S(1)} %iota_compare_fusion.2, ...), kind=kOutput, calls=%fused_computation.9.clone.1 | convolution fusion | flops 140509184 | bytes 3784708 | tf_op jit(solution)/shard_map/while/body/eval_jaxpr/khtu,kuhp->kthp/dot_general | solution.py:74
  135.2 1.1 constant_dynamic-slice_fusion.7
  136.3 3.7 %fusion.61 = f32[5,8,256,2,64]{2,4,3,1,0:T(8,128)} fusion(f32[5,8,256,2,64]{2,4,3,1,0:T(8,128)} %get-tuple-element.280, s32[]{:T(128)S(6)} %copy.124, f32[8,2,256]{2,1,0:T(2,128)S(1)} %bitcast.222, f32[8,256,256]{2,1,0:T(8,128)} %get-tuple-element.290, f32[8,2,256]{2,1,0:T(2,128)S(1)} %bitcast.223, pred[256,256]{1,0:T(8,128)(4,1)S(1)} %iota_compare_fusion.2, ...), kind=kOutput, calls=%fused_computation.9.clone.1 | convolution fusion | flops 140509184 | bytes 3784708 | tf_op jit(solution)/shard_map/while/body/eval_jaxpr/khtu,kuhp->kthp/dot_general | solution.py:74
  140.1 1.1 constant_dynamic-slice_fusion.7
  141.2 3.7 %fusion.61 = f32[5,8,256,2,64]{2,4,3,1,0:T(8,128)} fusion(f32[5,8,256,2,64]{2,4,3,1,0:T(8,128)} %get-tuple-element.280, s32[]{:T(128)S(6)} %copy.124, f32[8,2,256]{2,1,0:T(2,128)S(1)} %bitcast.222, f32[8,256,256]{2,1,0:T(8,128)} %get-tuple-element.290, f32[8,2,256]{2,1,0:T(2,128)S(1)} %bitcast.223, pred[256,256]{1,0:T(8,128)(4,1)S(1)} %iota_compare_fusion.2, ...), kind=kOutput, calls=%fused_computation.9.clone.1 | convolution fusion | flops 140509184 | bytes 3784708 | tf_op jit(solution)/shard_map/while/body/eval_jaxpr/khtu,kuhp->kthp/dot_general | solution.py:74
  145.0 5.5 %copy.76 = f32[8,256,5,2,64]{1,4,3,2,0:T(8,128)} copy(f32[8,256,5,2,64]{1,4,3,0,2:T(8,128)} %bitcast.211) | data formatting | bytes 10485760 | tf_op jit(solution)/shard_map/transpose | solution.py:100
  150.5 7.9 %all-gather.2 = f32[4,1,10]{2,1,0:T(1,128)S(1)} all-gather(f32[1,1,10]{2,1,0:T(1,128)S(1)} %copy-done.26), channel_id=1, replica_groups=mesh['seq_0'=4,'seq_1'=8,'head'=8] {'seq_0'}, dimensions={0}, use_global_device_ids=true | all-gather | bytes 200 | tf_op jit(solution)/shard_map/all_gather | solution.py:34
  158.5 2.7 %fusion.27 = f32[10,64,128]{2,1,0:T(8,128)S(1)} fusion(f32[4,10,64,128]{3,2,1,0:T(8,128)} %all-gather.9.cloned.1.call-done, f32[1,10,64,128]{3,2,1,0:T(8,128)S(1)} %copy-done.5, f32[1,10,64,128]{3,2,1,0:T(8,128)} %get-tuple-element.159, f32[80,64,128]{2,1,0:T(8,128)} %all-gather.11.cloned.1.call-done, f32[10]{0:T(128)S(1)} %copy-done.23, ...), kind=kLoop, calls=%fused_computation.48 | loop fusion | flops 2621440 | bytes 4260292 | tf_op jit(solution)/shard_map/mul | solution.py:120
  161.3 6.4 %fusion.19 = f32[8,256,10,64]{1,3,2,0:T(8,128)S(1)} fusion(f32[8,256,10,64]{1,3,2,0:T(8,128)} %bitcast.208, f32[8,256,10,64]{1,0,3,2:T(8,128)} %bitcast.203, f32[8,256,10]{1,2,0:T(8,128)S(1)} %copy-done.9, f32[10]{0:T(128)S(1)} %copy-done.27, bf16[8,256,128,1]{2,1,3,0:T(8,128)(2,1)S(1)} %bitcast.213, f32[8,10,64,128]{3,2,1,0:T(8,128)S(1)} %copy-done.6, ...), kind=kOutput, calls=%fused_computation.34 | convolution fusion | flops 342753280 | bytes 19284328 | tf_op jit(solution)/shard_map/ktn,khpn->kthp/dot_general | solution.py:123
  167.7 3.3 %copy.83 = f32[8,256,10,64]{1,0,3,2:T(8,128)S(1)} copy(f32[8,256,10,64]{1,3,2,0:T(8,128)S(1)} %fusion.19) | data formatting | bytes 10485760 | tf_op jit(solution)/shard_map/add | solution.py:124
  171.0 2.5 %copy.98 = f32[80,8,8,256]{3,1,2,0:T(8,128)S(1)} copy(f32[80,8,8,256]{3,2,1,0:T(8,128)S(1)} %bitcast.206) | data formatting | bytes 10485760
  173.5 2.3 %copy-done.1 = f32[80,8,8,256]{3,1,2,0:T(8,128)} copy-done((f32[80,8,8,256]{3,1,2,0:T(8,128)}, f32[80,8,8,256]{3,1,2,0:T(8,128)S(1)}, u32[]{:S(2)}) %copy-start.1) | copy-done | bytes 5242904
  175.8 1.7 multiply_reduce_fusion
  178.2 9.8 %all-to-all-start = ((f32[8,1,2048]{2,1,0:T(1,128)}), f32[8,1,2048]{2,1,0:T(1,128)S(1)}, u32[]{:S(2)}, u32[]{:S(2)}) async-start(f32[8,1,2048]{2,1,0:T(1,128)} %broadcast_in_dim.40), calls=%async_computation | async-start | bytes 131072 | tf_op jit(solution)/shard_map/all_to_all | solution.py:46
  188.8 4.1 %all-to-all-done = f32[8,1,2048]{2,1,0:T(1,128)S(1)} async-done(((f32[8,1,2048]{2,1,0:T(1,128)}), f32[8,1,2048]{2,1,0:T(1,128)S(1)}, u32[]{:S(2)}, u32[]{:S(2)}) %all-to-all-start) | async-done | bytes 65568 | tf_op jit(solution)/shard_map/all_to_all | solution.py:46
  192.9 5.2 %multiply_convert_fusion.6 = bf16[2048,640]{0,1:T(8,128)(2,1)} fusion(f32[640]{0:T(1024)S(1)} %dynamic_slice.30, f32[2048]{0:T(1024)S(1)} %add_rsqrt_fusion, f32[2048,640]{0,1:T(8,128)} %bitcast.205, bf16[2048,640]{0,1:T(8,128)(2,1)S(1)} %copy.84), kind=kLoop, calls=%fused_computation.35 | loop fusion | flops 11796480 | bytes 10496512 | tf_op jit(solution)/shard_map/convert_element_type | solution.py:148
  198.1 4.4 %copy.86 = bf16[2048,640]{1,0:T(8,128)(2,1)} copy(bf16[2048,640]{0,1:T(8,128)(2,1)} %multiply_convert_fusion.6) | data formatting | bytes 5242880 | tf_op jit(solution)/shard_map/convert_element_type | solution.py:148
  (128 shorter events, 16.0 us)
Async XLA Ops:
  6.5 10.4 %copy-start.3 = (bf16[2048,640]{1,0:T(8,128)(2,1)S(1)}, bf16[2048,640]{1,0:T(8,128)(2,1)}, u32[]{:S(2)}) copy-start(bf16[2048,640]{1,0:T(8,128)(2,1)} %param.12) | copy-start | bytes 7864324
  6.5 32.6 %all-gather.7.cloned.1.call-start = ((), (), s32[]{:S(2)}) async-start(), calls=%async_computation.1 | async-start | bytes 1179648 | tf_op jit(solution)/shard_map/all_gather | solution.py:19
  8.3 109.4 %all-gather.11.cloned.1.call-start = ((), (), s32[]{:S(2)}) async-start(), calls=%async_computation.3 | async-start | bytes 2949120 | tf_op jit(solution)/shard_map/all_gather | solution.py:34
  9.3 16.1 %copy-start.7 = (f32[2,8,8,256]{3,2,1,0:T(8,128)}, f32[2,8,8,256]{3,2,1,0:T(8,128)S(1)}, u32[]{:S(2)}) copy-start(f32[2,8,8,256]{3,2,1,0:T(8,128)S(1)} %copy.95) | copy-start | bytes 393220
  25.4 2.3 %copy-start = (f32[80,8,8,256]{3,2,1,0:T(8,128)}, f32[80,8,8,256]{3,2,1,0:T(8,128)S(1)}, u32[]{:S(2)}) copy-start(f32[80,8,8,256]{3,2,1,0:T(8,128)S(1)} %copy.97) | copy-start | bytes 15728644
  40.4 2.4 %copy-start.4 = (bf16[2048,128]{1,0:T(8,128)(2,1)}, bf16[2048,128]{1,0:T(8,128)(2,1)S(1)}, u32[]{:S(2)}) copy-start(bf16[2048,128]{1,0:T(8,128)(2,1)S(1)} %get-tuple-element.167) | copy-start | bytes 1572868
  77.8 0.7 copy-start.2
  77.8 3.9 %copy-start.8 = (f32[2,8,8,256]{3,2,1,0:T(8,128)S(1)}, f32[2,8,8,256]{3,2,1,0:T(8,128)}, u32[]{:S(2)}) copy-start(f32[2,8,8,256]{3,2,1,0:T(8,128)} %copy-done.7) | copy-start | bytes 393220
  78.6 79.9 %all-gather.9.cloned.1.call-start = ((), (), s32[]{:S(2)}) async-start(), calls=%async_computation.2 | async-start | bytes 1638400 | tf_op jit(solution)/shard_map/all_gather | solution.py:34
  78.6 5.5 %copy-start.10 = (f32[8,256,10]{1,0,2:T(8,128)S(1)}, f32[8,256,10]{1,0,2:T(8,128)}, u32[]{:S(2)}) copy-start(f32[8,256,10]{1,0,2:T(8,128)} %get-tuple-element.160) | copy-start | bytes 245764
  78.6 6.2 %copy-start.28 = (f32[80]{0:T(128)S(1)}, f32[80]{0:T(128)}, u32[]{:S(2)}) copy-start(f32[80]{0:T(128)} %param.18) | copy-start | bytes 964
  81.7 6.7 %copy-start.29 = (u32[256]{0:T(256)S(1)}, u32[256]{0:T(256)}, u32[]{:S(2)}) copy-start(u32[256]{0:T(256)} %constant.87) | copy-start | bytes 3076
  81.7 8.0 %copy-start.11 = (f32[10]{0:T(128)S(1)}, f32[10]{0:T(128)}, u32[]{:S(2)}) copy-start(f32[10]{0:T(128)} %get-tuple-element.79) | copy-start | bytes 124
  106.2 14.2 %copy-start.12 = (f32[10]{0:T(128)}, f32[10]{0:T(128)S(1)}, u32[]{:S(2)}) copy-start(f32[10]{0:T(128)S(1)} %get-tuple-element.174) | copy-start | bytes 124
  106.2 14.3 %copy-start.14 = (f32[10]{0:T(128)}, f32[10]{0:T(128)S(1)}, u32[]{:S(2)}) copy-start(f32[10]{0:T(128)S(1)} %get-tuple-element.175) | copy-start | bytes 124
  106.2 14.3 %copy-start.16 = (f32[10]{0:T(128)}, f32[10]{0:T(128)S(1)}, u32[]{:S(2)}) copy-start(f32[10]{0:T(128)S(1)} %get-tuple-element.177) | copy-start | bytes 124
  106.2 14.3 %copy-start.18 = (f32[10]{0:T(128)}, f32[10]{0:T(128)S(1)}, u32[]{:S(2)}) copy-start(f32[10]{0:T(128)S(1)} %get-tuple-element.178) | copy-start | bytes 124
  106.2 14.3 %copy-start.20 = (f32[10]{0:T(128)}, f32[10]{0:T(128)S(1)}, u32[]{:S(2)}) copy-start(f32[10]{0:T(128)S(1)} %get-tuple-element.179) | copy-start | bytes 124
  106.2 14.3 %copy-start.22 = (f32[10]{0:T(128)}, f32[10]{0:T(128)S(1)}, u32[]{:S(2)}) copy-start(f32[10]{0:T(128)S(1)} %get-tuple-element.181) | copy-start | bytes 124
  144.9 5.6 %copy-start.24 = (f32[8,10]{1,0:T(8,128)S(1)}, f32[8,10]{1,0:T(8,128)}, u32[]{:S(2)}) copy-start(f32[8,10]{1,0:T(8,128)} %get-tuple-element.78) | copy-start | bytes 964
  144.9 5.6 %copy-start.26 = (f32[1,1,10]{2,1,0:T(1,128)S(1)}, f32[1,1,10]{2,1,0:T(1,128)}, u32[]{:S(2)}) copy-start(f32[1,1,10]{2,1,0:T(1,128)} %get-tuple-element.173) | copy-start | bytes 124
  144.9 13.6 %copy-start.5 = (f32[1,10,64,128]{3,2,1,0:T(8,128)S(1)}, f32[1,10,64,128]{3,2,1,0:T(8,128)}, u32[]{:S(2)}) copy-start(f32[1,10,64,128]{3,2,1,0:T(8,128)} %get-tuple-element.158) | copy-start | bytes 983044
  144.9 13.6 %copy-start.13 = (f32[10]{0:T(128)S(1)}, f32[10]{0:T(128)}, u32[]{:S(2)}) copy-start(f32[10]{0:T(128)} %copy-done.12) | copy-start | bytes 124
  144.9 13.6 %copy-start.15 = (f32[10]{0:T(128)S(1)}, f32[10]{0:T(128)}, u32[]{:S(2)}) copy-start(f32[10]{0:T(128)} %copy-done.14) | copy-start | bytes 124
  144.9 13.6 %copy-start.17 = (f32[10]{0:T(128)S(1)}, f32[10]{0:T(128)}, u32[]{:S(2)}) copy-start(f32[10]{0:T(128)} %copy-done.16) | copy-start | bytes 124
  144.9 13.6 %copy-start.19 = (f32[10]{0:T(128)S(1)}, f32[10]{0:T(128)}, u32[]{:S(2)}) copy-start(f32[10]{0:T(128)} %copy-done.18) | copy-start | bytes 124
  144.9 13.6 %copy-start.21 = (f32[10]{0:T(128)S(1)}, f32[10]{0:T(128)}, u32[]{:S(2)}) copy-start(f32[10]{0:T(128)} %copy-done.20) | copy-start | bytes 124
  144.9 13.6 %copy-start.23 = (f32[10]{0:T(128)S(1)}, f32[10]{0:T(128)}, u32[]{:S(2)}) copy-start(f32[10]{0:T(128)} %copy-done.22) | copy-start | bytes 124
  145.0 13.6 %copy-start.25 = (f32[10]{0:T(128)S(1)}, f32[10]{0:T(128)}, u32[]{:S(2)}) copy-start(f32[10]{0:T(128)} %get-tuple-element.156) | copy-start | bytes 124
  150.5 10.8 %copy-start.27 = (f32[10]{0:T(128)S(1)}, f32[10]{0:T(128)}, u32[]{:S(2)}) copy-start(f32[10]{0:T(128)} %dynamic_slice.29) | copy-start | bytes 124
  158.4 2.9 %copy-start.6 = (f32[8,10,64,128]{3,2,1,0:T(8,128)S(1)}, f32[8,10,64,128]{3,2,1,0:T(8,128)}, u32[]{:S(2)}) copy-start(f32[8,10,64,128]{3,2,1,0:T(8,128)} %get-tuple-element.81) | copy-start | bytes 7864324
  158.4 2.9 %copy-start.9 = (f32[8,256,10]{1,2,0:T(8,128)S(1)}, f32[8,256,10]{1,2,0:T(8,128)}, u32[]{:S(2)}) copy-start(f32[8,256,10]{1,2,0:T(8,128)} %copy.79) | copy-start | bytes 245764
  173.5 2.3 %copy-start.1 = (f32[80,8,8,256]{3,1,2,0:T(8,128)}, f32[80,8,8,256]{3,1,2,0:T(8,128)S(1)}, u32[]{:S(2)}) copy-start(f32[80,8,8,256]{3,1,2,0:T(8,128)S(1)} %copy.98) | copy-start | bytes 15728644
  178.2 14.6 %all-to-all-start = ((f32[8,1,2048]{2,1,0:T(1,128)}), f32[8,1,2048]{2,1,0:T(1,128)S(1)}, u32[]{:S(2)}, u32[]{:S(2)}) async-start(f32[8,1,2048]{2,1,0:T(1,128)} %broadcast_in_dim.40), calls=%async_computation | async-start | bytes 131072 | tf_op jit(solution)/shard_map/all_to_all | solution.py:46
Sparse Core Ops, SparseCore 0:
  9.2 29.9 all-gather.6
  78.7 38.9 all-gather.10
  120.6 27.7 all-gather.8
where the time goes:
time: 211 us; the launch traced here: 209 us
  local copies, waits for them, and re-layouts  60.7 us (29%)
  other arithmetic  47.4 us (22%)
  matrix products  30.1 us (14%)
  waiting for transfers between devices  23.6 us (11%)
  blocking collectives  22.8 us (11%)
  between operations  14.3 us (7%)
  starting transfers between devices  9.86 us (5%)
    unnamed x70, local copies, waits for them, and re-layouts  22.1 us
    dot_general x5, matrix products, intra_block(): jnp.einsum('khtu,kuhp->kthp', mixing, values, preferred_element_type=jnp....  18.6 us
    unnamed x1, blocking collectives  14.9 us
    add x9, other arithmetic, combine(): jnp.exp(later[0])[:, None, None] * earlier[1] + later[1]  11.3 us
    all_gather x1, waiting for transfers between devices, side_by_side(): filled = lax.all_gather(both, axis, axis=dim, tiled=True)  10.9 us
    exp x10, other arithmetic, combine(): jnp.exp(later[0])[:, None, None] * earlier[1] + later[1]  10.7 us
    dynamic_update_slice x8, local copies, waits for them, and re-layouts, within_device(): return lax.scan(advance, start, (totals, states))  10.3 us
    all_to_all x1, starting transfers between devices, from_everyone(): lax.all_to_all(jnp.broadcast_to(value[None], (devices, *value.shape)), ax...  9.77 us
  transfers between devices with their start and end apart: 4, of which 3 were waited for; matrix products, arithmetic and copies ran while one was open for 30% of the time, Pallas kernels for 0%

commit v1 on v0

v1 whole, which is shorter than its diff:
```python
import jax
import jax.numpy as jnp
from jax import lax
from jax.experimental import pallas as pl
from jax.experimental.pallas import tpu as pltpu
from jax.sharding import Mesh
from jax.sharding import PartitionSpec as P

HEADS = 80
HEAD_DIM = 64
STATE = 128
INNER = HEADS * HEAD_DIM
EPS = 1e-05

NY, NZ, NX, NC = 4, 8, 4, 2
NH = NX * NC
HL = HEADS // NH
PAIRS = HL // 2
WIDTH = HL * HEAD_DIM
TOKENS = 2048
CH = 128
NCH = TOKENS // CH
BLK = TOKENS // NH
HP = 16
SLICE = STATE // NZ
GROUPS = 2
GCH = NCH // GROUPS

LOG2E = 1.4426950408889634
MESH_ID = pl.DeviceIdType.MESH
F32 = jnp.float32
BF16 = jnp.bfloat16
AXES = ("y", "z", "x", "c")


def mm(a, b, ca=1, cb=0):
    return lax.dot_general(a, b, (((ca,), (cb,)), ((), ())), preferred_element_type=F32)


def split2(v):
    hi = v.astype(BF16)
    return hi, (v - hi.astype(F32)).astype(BF16)


def split3(v):
    hi = v.astype(BF16)
    rest = v - hi.astype(F32)
    mid = rest.astype(BF16)
    return hi, mid, (rest - mid.astype(F32)).astype(BF16)


def kernel(
    x_hbm, z_hbm, raw_hbm, decay_ref, b_hbm, c_hbm, skip_ref, gain_ref, out_ref,
    x_ref, z_ref, raw_ref, b_ref, c_ref, bt_ref, r_ref, q_ref, w_ref, wd_ref,
    tot_ref, off_ref, acc_ref, sb_ref, a_ref, e_ref,
    s_in, p_ref, d_mine, d_all, dl_mine, dl_all, t_mine, t_all, cs_ref, carry_ref, sq_ref,
    load_sem, bs_sem, br_sem, cs_sem, cr_sem, ds_sem, dr_sem, dls_sem, dlr_sem,
    s1_sem, r1_sem, s2_sem, r2_sem, s3_sem, r3_sem, sqs_sem, sqr_sem,
):
    y, z, xx, cc = (lax.axis_index(n) for n in AXES)
    head = xx * NC + cc

    def to(ny=None, nz=None, nx=None, nc=None):
        return (
            y if ny is None else ny,
            z if nz is None else nz,
            xx if nx is None else nx,
            cc if nc is None else nc,
        )

    def remote(src, dst, ssem, rsem, dev):
        return pltpu.make_async_remote_copy(
            src_ref=src, dst_ref=dst, send_sem=ssem, recv_sem=rsem,
            device_id=dev, device_id_type=MESH_ID,
        )

    def rows(slot):
        return pl.ds(pl.multiple_of(slot * BLK, BLK), BLK)

    load_b = pltpu.make_async_copy(b_hbm, b_ref.at[rows(head)], load_sem.at[0])
    load_c = pltpu.make_async_copy(c_hbm, c_ref.at[rows(head)], load_sem.at[1])
    load_raw = pltpu.make_async_copy(raw_hbm, raw_ref, load_sem.at[2])
    load_x = pltpu.make_async_copy(x_hbm, x_ref, load_sem.at[3])
    load_z = pltpu.make_async_copy(z_hbm, z_ref, load_sem.at[4])
    for c in (load_b, load_c, load_raw, load_x, load_z):
        c.start()

    zp = [lax.rem(z + o, NZ) for o in range(1, NZ)]
    zm = [lax.rem(z + NZ - o, NZ) for o in range(1, NZ)]
    yp = [lax.rem(y + o, NY) for o in range(1, NY)]
    ym = [lax.rem(y + NY - o, NY) for o in range(1, NY)]
    hp = [lax.rem(head + o, NH) for o in range(1, NH)]
    hm = [lax.rem(head + NH - o, NH) for o in range(1, NH)]

    barrier = pltpu.get_barrier_semaphore()
    for k in zp:
        pl.semaphore_signal(barrier, inc=1, device_id=to(nz=k), device_id_type=MESH_ID)
    for k in yp:
        pl.semaphore_signal(barrier, inc=1, device_id=to(ny=k), device_id_type=MESH_ID)
    for k in hp:
        pl.semaphore_signal(
            barrier, inc=1, device_id=to(nx=k // NC, nc=lax.rem(k, NC)), device_id_type=MESH_ID
        )
    pl.semaphore_wait(barrier, (NZ - 1) + (NY - 1) + (NH - 1))

    other = 1 - cc
    hops = (1, 3, 2)
    mine = head

    def gather_sends(ref, ssem, rsem):
        out = []
        for i, o in enumerate(hops):
            out.append(remote(
                ref.at[rows(mine)], ref.at[rows(mine)], ssem.at[1 + i], rsem.at[1 + i],
                to(nx=lax.rem(xx + o, NX)),
            ))
        out.append(remote(
            ref.at[rows(mine)], ref.at[rows(mine)], ssem.at[0], rsem.at[0], to(nc=other)
        ))
        return out

    def slot_of(i):
        k = lax.rem(i + 2, 3)
        hop = jnp.where(k == 0, 1, jnp.where(k == 1, 3, 2))
        chip = jnp.where(i == 0, xx, lax.rem(xx + NX - hop, NX))
        core = jnp.where((i >= 1) & (i <= 3), cc, other)
        return chip * NC + core

    def incoming(ref, ssem, rsem, i):
        at = rows(slot_of(i))
        return remote(ref.at[at], ref.at[at], ssem.at[i], rsem.at[i], to(nc=other))

    def forward(ref, ssem, rsem, i):
        at = rows(slot_of(i))
        return remote(ref.at[at], ref.at[at], ssem.at[i + 3], rsem.at[i + 3], to(nc=other))

    load_b.wait()
    b_sends = gather_sends(b_ref, bs_sem, br_sem)
    for c in b_sends:
        c.start()
    load_c.wait()
    c_sends = gather_sends(c_ref, cs_sem, cr_sem)
    for c in c_sends:
        c.start()

    load_raw.wait()
    eye = (
        lax.broadcasted_iota(jnp.int32, (HP, HL), 0) == lax.broadcasted_iota(jnp.int32, (HP, HL), 1)
    ).astype(F32).astype(BF16)
    raw = mm(eye, raw_ref[...], 1, 1)
    step = jnp.maximum(raw, 0.0) + jnp.log1p(jnp.exp(-jnp.abs(raw)))
    sub = lax.broadcasted_iota(jnp.int32, (HP, CH), 0)
    rate = jnp.zeros((HP, CH), F32)
    for h in range(HL):
        rate = jnp.where(sub == h, decay_ref[head * HL + h], rate)
    rate = jnp.where(sub < HL, -LOG2E * jnp.exp(rate), 0.0)
    steps = jnp.concatenate([step[:, k * CH:(k + 1) * CH] for k in range(NCH)], axis=0)
    decays = steps * jnp.concatenate([rate] * NCH, axis=0)
    upper = (
        lax.broadcasted_iota(jnp.int32, (CH, CH), 0) <= lax.broadcasted_iota(jnp.int32, (CH, CH), 1)
    ).astype(F32).astype(BF16)
    hi, mid, lo = split3(decays)
    run = mm(hi, upper) + mm(mid, upper) + mm(lo, upper)
    r_ref[...] = run
    q = run - jnp.log2(steps)
    q_ref[...] = q
    total = jnp.broadcast_to(run[:, CH - 1:CH], (NCH * HP, CH))
    w_ref[...] = jnp.exp2(total - q)
    after = jnp.zeros((HP, CH), F32)
    for k in reversed(range(NCH)):
        at = slice(k * HP, (k + 1) * HP)
        wd_ref[at, :] = jnp.exp2(after + (total[at] - q[at]))
        after = after + total[at]
    left1 = lax.broadcasted_iota(jnp.int32, (1, CH), 1) < HEAD_DIM

    def wide(v):
        return jnp.concatenate(
            [jnp.where(left1, v[2 * p:2 * p + 1], v[2 * p + 1:2 * p + 2]) for p in range(PAIRS)],
            axis=1,
        )

    d_row = wide(after)
    d_mine[...] = d_row
    d_sends = [
        remote(d_mine, d_all.at[z], ds_sem.at[i], dr_sem.at[i], to(nz=k)) for i, k in enumerate(zp)
    ]
    for c in d_sends:
        c.start()
    d_all[z] = d_row
    before = jnp.zeros((HP, CH), F32)
    for k in range(NCH):
        at = slice(k * HP, (k + 1) * HP)
        tot_ref[k] = jnp.exp2(wide(total[at]))
        off_ref[k] = jnp.exp2(wide(before))
        before = before + total[at]

    acc_ref[...] = jnp.zeros_like(acc_ref)
    left = lax.broadcasted_iota(jnp.int32, (CH, CH), 1) < HEAD_DIM
    load_x.wait()

    def add_block(slot):
        at = rows(slot)
        bt0 = b_ref[pl.ds(pl.multiple_of(slot * BLK, BLK), CH), :].astype(F32).T
        bt1 = b_ref[pl.ds(pl.multiple_of(slot * BLK + CH, CH), CH), :].astype(F32).T
        bt_ref[2 * slot] = bt0
        bt_ref[2 * slot + 1] = bt1
        base = pl.multiple_of(slot * 2 * HP, 2 * HP)
        w0 = wd_ref[pl.ds(base, HP), :]
        w1 = wd_ref[pl.ds(base + HP, HP), :]
        for p in range(PAIRS):
            cols = slice(p * CH, (p + 1) * CH)
            lhs = jnp.concatenate(
                [
                    jnp.concatenate(
                        [
                            (bt0 * w0[h:h + 1]).astype(BF16),
                            (bt1 * w1[h:h + 1]).astype(BF16),
                        ],
                        axis=1,
                    )
                    for h in (2 * p, 2 * p + 1)
                ],
                axis=0,
            )
            o = mm(lhs, x_ref[at, cols])
            acc_ref[:, cols] += jnp.where(left, o[:CH], o[CH:])

    add_block(mine)

    def gathered(i, _):
        incoming(b_ref, bs_sem, br_sem, i).wait_recv()

        @pl.when((i >= 1) & (i <= 3))
        def _():
            forward(b_ref, bs_sem, br_sem, i).start()

        add_block(slot_of(i))
        return 0

    lax.fori_loop(0, NH - 1, gathered, 0)

    def slc(k):
        return pl.ds(pl.multiple_of(k * SLICE, SLICE), SLICE)

    sb_ref[...] = acc_ref[...].astype(BF16)
    s_sends = [
        remote(sb_ref.at[slc(k)], s_in.at[z], s1_sem.at[i], r1_sem.at[i], to(nz=k))
        for i, k in enumerate(zp)
    ]
    for c in s_sends:
        c.start()
    s_in[z] = sb_ref[slc(z), :]

    for i, k in enumerate(zm):
        remote(d_mine, d_all.at[k], ds_sem.at[i], dr_sem.at[i], to(nz=k)).wait_recv()
    line = d_all[0]
    for k in range(1, NZ):
        line = line + d_all[k]
    dl_mine[...] = line
    dl_sends = [
        remote(dl_mine, dl_all.at[y], dls_sem.at[i], dlr_sem.at[i], to(ny=k))
        for i, k in enumerate(yp)
    ]
    for c in dl_sends:
        c.start()
    dl_all[y] = line

    for i in range(1, 4):
        incoming(c_ref, cs_sem, cr_sem, i).wait_recv()
        forward(c_ref, cs_sem, cr_sem, i).start()
    load_z.wait()
    for i in (0, 4, 5, 6):
        incoming(c_ref, cs_sem, cr_sem, i).wait_recv()

    acc_ref[...] = jnp.zeros_like(acc_ref)
    cap = jnp.where(
        lax.broadcasted_iota(jnp.int32, (CH, CH), 0) >= lax.broadcasted_iota(jnp.int32, (CH, CH), 1),
        1e3, -1e30,
    )

    def chunk(k, _):
        at = pl.ds(pl.multiple_of(k * CH, CH), CH)
        hat = pl.ds(pl.multiple_of(k * HP, HP), HP)
        bk, ck = b_ref[at, :], c_ref[at, :]
        scores = mm(ck, bk, 1, 1)
        bt = bt_ref[k]
        rc = r_ref[hat, :].T
        qk, wk = q_ref[hat, :], w_ref[hat, :]
        tot, off = tot_ref[k], off_ref[k]
        for p in range(PAIRS):
            cols = slice(p * CH, (p + 1) * CH)
            mix, ws, rb = [], [], []
            for h in (2 * p, 2 * p + 1):
                r = jnp.broadcast_to(rc[:, h:h + 1], (CH, CH))
                rb.append(r)
                m = jnp.exp2(jnp.minimum(r - qk[h:h + 1], cap)) * scores
                mix.append(m.astype(BF16))
                ws.append((bt * wk[h:h + 1]).astype(BF16))
            lhs = jnp.concatenate(
                [jnp.concatenate(mix, axis=1), jnp.concatenate(ws, axis=1)], axis=0
            )
            xp = x_ref[at, cols]
            zero = jnp.zeros_like(xp)
            rhs = jnp.concatenate([jnp.where(left, xp, zero), jnp.where(left, zero, xp)], axis=0)
            o = mm(lhs, rhs)
            state = acc_ref[:, cols]
            inter = mm(ck, state.astype(BF16))
            er = jnp.exp2(jnp.where(left, rb[0], rb[1]))
            first = head * HL + 2 * p
            skip = jnp.where(left1, skip_ref[first], skip_ref[first + 1])
            zv = z_ref[at, cols].astype(F32)
            gate = zv * (0.5 + 0.5 * jnp.tanh(0.5 * zv))
            a_ref[at, cols] = (o[:CH] + er * inter + skip * xp.astype(F32)) * gate
            e_ref[at, cols] = er * gate * off[:, cols]
            acc_ref[:, cols] = state * tot[:, cols] + o[CH:]
        return 0

    lax.fori_loop(0, 6, chunk, 0)

    for i, k in enumerate(zm):
        remote(sb_ref.at[slc(k)], s_in.at[k], s1_sem.at[i], r1_sem.at[i], to(nz=k)).wait_recv()
    pre = jnp.zeros((SLICE, WIDTH), F32)
    for k in range(NZ):
        p_ref[k] = pre
        pre = pre * jnp.exp2(d_all[k]) + s_in[k].astype(F32)
    t_mine[...] = pre.astype(BF16)
    t_sends = [
        remote(t_mine, t_all.at[y], s2_sem.at[i], r2_sem.at[i], to(ny=k)) for i, k in enumerate(yp)
    ]
    for c in t_sends:
        c.start()
    t_all[y] = pre.astype(BF16)

    lax.fori_loop(6, 10, chunk, 0)

    for i, k in enumerate(ym):
        remote(dl_mine, dl_all.at[k], dls_sem.at[i], dlr_sem.at[i], to(ny=k)).wait_recv()
        remote(t_mine, t_all.at[k], s2_sem.at[i], r2_sem.at[i], to(ny=k)).wait_recv()
    into = jnp.zeros((SLICE, WIDTH), F32)
    for k in range(NY - 1):
        into = jnp.where(k < y, into * jnp.exp2(dl_all[k]) + t_all[k].astype(F32), into)
    upto = jnp.zeros((1, WIDTH), F32)
    for k in range(NZ):
        cs_ref[k] = (p_ref[k] + jnp.exp2(upto) * into).astype(BF16)
        upto = upto + d_all[k]
    k_sends = [
        remote(cs_ref.at[k], carry_ref.at[slc(z)], s3_sem.at[i], r3_sem.at[i], to(nz=k))
        for i, k in enumerate(zp)
    ]
    for c in k_sends:
        c.start()
    carry_ref[slc(z), :] = cs_ref[z]

    lax.fori_loop(10, NCH, chunk, 0)

    for i, k in enumerate(zm):
        remote(cs_ref.at[k], carry_ref.at[slc(k)], s3_sem.at[i], r3_sem.at[i], to(nz=k)).wait_recv()

    ones8 = jnp.ones((8, 2 * CH), F32).astype(BF16)

    def finish(k, _):
        at = pl.ds(pl.multiple_of(k * CH, CH), CH)
        ck = c_ref[at, :]
        part = jnp.zeros((CH, CH), F32)
        for p in range(PAIRS):
            cols = slice(p * CH, (p + 1) * CH)
            g = a_ref[at, cols] + e_ref[at, cols] * mm(ck, carry_ref[:, cols])
            a_ref[at, cols] = g
            part = part + g * g
        s = mm(ones8, jnp.concatenate(split2(part), axis=1), 1, 1)
        sq_ref[k, head] = s[0:1]
        return 0

    def group(g):
        return pl.ds(g * GCH, GCH)

    q_sends = []
    for g in range(GROUPS):
        lax.fori_loop(g * GCH, (g + 1) * GCH, finish, 0)
        for i, k in enumerate(hp):
            c = remote(
                sq_ref.at[group(g), head], sq_ref.at[group(g), head], sqs_sem.at[g, i], sqr_sem.at[g, i],
                to(nx=k // NC, nc=lax.rem(k, NC)),
            )
            c.start()
            q_sends.append(c)

    ones16 = jnp.ones((2 * NH, CH), F32).astype(BF16)
    gains = [gain_ref[pl.ds(head * PAIRS + p, 1), :] for p in range(PAIRS)]

    def scale(k, _):
        at = pl.ds(pl.multiple_of(k * CH, CH), CH)
        hi, lo = split2(sq_ref[k].reshape(NH, CH))
        both = jnp.concatenate([hi.astype(F32), lo.astype(F32)], axis=0).astype(BF16)
        s = mm(both, ones16, 0, 0)
        f = lax.rsqrt(s * (1.0 / INNER) + EPS)
        for p in range(PAIRS):
            cols = slice(p * CH, (p + 1) * CH)
            out_ref[at, cols] = (a_ref[at, cols] * f * gains[p]).astype(BF16)
        return 0

    for g in range(GROUPS):
        for i, k in enumerate(hm):
            remote(
                sq_ref.at[group(g), k], sq_ref.at[group(g), k], sqs_sem.at[g, i], sqr_sem.at[g, i],
                to(nx=k // NC, nc=lax.rem(k, NC)),
            ).wait_recv()
        lax.fori_loop(g * GCH, (g + 1) * GCH, scale, 0)

    for c in b_sends + c_sends + d_sends + s_sends + dl_sends + t_sends + k_sends + q_sends:
        c.wait_send()
    for i in range(1, 4):
        forward(b_ref, bs_sem, br_sem, i).wait_send()
        forward(c_ref, cs_sem, cr_sem, i).wait_send()


def on_device(x, zg, raw, decay, b, c, skip, gain):
    any_ = pl.BlockSpec(memory_space=pl.ANY)
    smem = pl.BlockSpec(memory_space=pltpu.SMEM)
    vmem = pl.BlockSpec(memory_space=pltpu.VMEM)
    dma = pltpu.SemaphoreType.DMA
    v = pltpu.VMEM
    return pl.pallas_call(
        kernel,
        out_shape=jax.ShapeDtypeStruct((TOKENS, WIDTH), BF16),
        in_specs=[any_, any_, any_, smem, any_, any_, smem, vmem],
        out_specs=vmem,
        scratch_shapes=[
            v((TOKENS, WIDTH), BF16),
            v((TOKENS, WIDTH), BF16),
            v((TOKENS, HL), BF16),
            v((TOKENS, STATE), BF16),
            v((TOKENS, STATE), BF16),
            v((NCH, STATE, CH), F32),
            v((NCH * HP, CH), F32),
            v((NCH * HP, CH), F32),
            v((NCH * HP, CH), F32),
            v((NCH * HP, CH), F32),
            v((NCH, 1, WIDTH), F32),
            v((NCH, 1, WIDTH), F32),
            v((STATE, WIDTH), F32),
            v((STATE, WIDTH), BF16),
            v((TOKENS, WIDTH), F32),
            v((TOKENS, WIDTH), F32),
            v((NZ, SLICE, WIDTH), BF16),
            v((NZ, SLICE, WIDTH), F32),
            v((1, WIDTH), F32),
            v((NZ, 1, WIDTH), F32),
            v((1, WIDTH), F32),
            v((NY, 1, WIDTH), F32),
            v((SLICE, WIDTH), BF16),
            v((NY, SLICE, WIDTH), BF16),
            v((NZ, SLICE, WIDTH), BF16),
            v((STATE, WIDTH), BF16),
            v((NCH, NH, 1, CH), F32),
            dma((5,)),
            dma((NH - 1,)), dma((NH - 1,)),
            dma((NH - 1,)), dma((NH - 1,)),
            dma((NZ - 1,)), dma((NZ - 1,)),
            dma((NY - 1,)), dma((NY - 1,)),
            dma((NZ - 1,)), dma((NZ - 1,)),
            dma((NY - 1,)), dma((NY - 1,)),
            dma((NZ - 1,)), dma((NZ - 1,)),
            dma((GROUPS, NH - 1)), dma((GROUPS, NH - 1)),
        ],
        compiler_params=pltpu.CompilerParams(
            collective_id=0, has_side_effects=True, vmem_limit_bytes=48 * 1024 * 1024
        ),
        name="ssd",
    )(x, zg, raw, decay, b, c, skip, gain.reshape(INNER // CH, CH))


def solution(mesh):
    finer = Mesh(mesh.devices.reshape(NY, NZ, NX, NC), AXES)
    seq, head = ("y", "z"), ("x", "c")
    placed = (
        P(seq, head), P(seq, head), P(seq, head), P(),
        P(seq + head, None), P(seq + head, None), P(), P(),
    )
    return jax.shard_map(
        on_device, mesh=finer, in_specs=placed, out_specs=P(seq, head), check_vma=False
    )
```

time: 211 us -> 55.9 us (0.26)
  local copies, waits for them, and re-layouts: 60.7 us -> 8.08 us
  Pallas kernels: 0 us -> 47.4 us
  other arithmetic: 47.4 us -> 0 us
  matrix products: 30.1 us -> 0 us
  waiting for transfers between devices: 23.6 us -> 0 us
  blocking collectives: 22.8 us -> 0 us
  between operations: 14.3 us -> 0.02 us
  starting transfers between devices: 9.86 us -> 0 us
    pallas_call x0 -> x1, Pallas kernels: none -> 47.4 us  [on_device(): pl.pallas_call(kernel, out_shape=jax.ShapeDtypeStruct((TOKENS, WIDTH), BF...]
    dot_general x8 -> x0, matrix products: 30.1 us -> none  [the longest x5 18.6 us: intra_block(): jnp.einsum('khtu,kuhp->kthp', mixing, values, preferred_element_type=jnp....]
    all_gather x3 -> x0, waiting for transfers between devices: 19.5 us -> none  [the longest x1 10.9 us: side_by_side(): filled = lax.all_gather(both, axis, axis=dim, tiled=True)]
    unnamed x1 -> x0, blocking collectives: 14.9 us -> none
    unnamed x70 -> x14, local copies, waits for them, and re-layouts: 22.1 us -> 8.08 us
    add x9 -> x0, other arithmetic: 11.3 us -> none  [combine(): jnp.exp(later[0])[:, None, None] * earlier[1] + later[1]]
    exp x10 -> x0, other arithmetic: 10.7 us -> none  [combine(): jnp.exp(later[0])[:, None, None] * earlier[1] + later[1]]
    dynamic_update_slice x8 -> x0, local copies, waits for them, and re-layouts: 10.3 us -> none  [within_device(): return lax.scan(advance, start, (totals, states))]
  transfers between devices with their start and end apart: 4 -> 0, of which waited for: 3 -> 0; matrix products, arithmetic and copies ran while one was open for 30% -> 0% of each run, Pallas kernels for 0% -> 0%
where the time goes in v1:
time: 55.9 us; the launch traced here: 55.5 us
  Pallas kernels  47.4 us (85%)
  local copies, waits for them, and re-layouts  8.08 us (14%)
    pallas_call x1, Pallas kernels, on_device(): pl.pallas_call(kernel, out_shape=jax.ShapeDtypeStruct((TOKENS, WIDTH), BF...  47.4 us
    unnamed x14, local copies, waits for them, and re-layouts  8.08 us

profile of v1, /device:TPU:1, one launch (start us, length us, event | category | flops | bytes accessed | tf_op | source)
XLA Modules:
  0.0 55.5 jit_solution(18301382218070539426)
XLA Ops:
  0.0 1.1 %copy.9.raw_hbm = bf16[2048,10]{1,0:T(8,128)(2,1)S(1)} copy(bf16[2048,10]{0,1:T(8,128)(2,1)} %param.10) | data formatting | bytes 81920 | tf_op args[2]
  1.1 0.0 copy-start
  1.2 1.7 %copy-done = bf16[2048,640]{1,0:T(8,128)(2,1)S(1)} copy-done((bf16[2048,640]{1,0:T(8,128)(2,1)S(1)}, bf16[2048,640]{1,0:T(8,128)(2,1)}, u32[]{:S(2)}) %copy-start) | copy-done | bytes 2621464
  2.9 0.0 copy-start.1
  2.9 0.8 %copy-done.1 = bf16[256,128]{1,0:T(8,128)(2,1)S(1)} copy-done((bf16[256,128]{1,0:T(8,128)(2,1)S(1)}, bf16[256,128]{1,0:T(8,128)(2,1)}, u32[]{:S(2)}) %copy-start.1) | copy-done | bytes 65560
  3.7 0.0 copy-start.2
  3.7 0.8 %copy-done.2 = bf16[256,128]{1,0:T(8,128)(2,1)S(1)} copy-done((bf16[256,128]{1,0:T(8,128)(2,1)S(1)}, bf16[256,128]{1,0:T(8,128)(2,1)}, u32[]{:S(2)}) %copy-start.2) | copy-done | bytes 65560
  4.6 0.0 copy-start.3
  4.6 0.7 %copy-done.3 = f32[5120]{0:T(1024)S(1)} copy-done((f32[5120]{0:T(1024)S(1)}, f32[5120]{0:T(1024)}, u32[]{:S(2)}) %copy-start.3) | copy-done | bytes 20504
  5.3 0.0 copy-start.4
  5.3 0.7 %copy-done.4 = f32[80]{0:T(128)S(1)} copy-done((f32[80]{0:T(128)S(1)}, f32[80]{0:T(128)}, u32[]{:S(2)}) %copy-start.4) | copy-done | bytes 344
  5.9 0.0 copy-start.5
  6.0 0.7 %copy-done.5 = f32[80]{0:T(128)S(1)} copy-done((f32[80]{0:T(128)S(1)}, f32[80]{0:T(128)}, u32[]{:S(2)}) %copy-start.5) | copy-done | bytes 344
  6.6 47.4 %ssd.1 = bf16[2048,640]{1,0:T(8,128)(2,1)S(1)} custom-call(bf16[2048,640]{1,0:T(8,128)(2,1)S(1)} %copy-done, bf16[2048,640]{1,0:T(8,128)(2,1)} %z_hbm.1, bf16[2048,10]{1,0:T(8,128)(2,1)S(1)} %copy.9.raw_hbm, f32[80]{0:T(128)S(1)} %copy-done.4, bf16[256,128]{1,0:T(8,128)(2,1)S(1)} %copy-done.1, bf16[256,128]{1,0:T(8,128)(2,1)S(1)} %copy-done.2, ...), custom_call_target="tpu_custom_call" | custom-call | tf_op jit(solution)/shard_map/ssd/pallas_call | solution.py:423
  54.0 1.5 %copy.11 = bf16[2048,640]{1,0:T(8,128)(2,1)} copy(bf16[2048,640]{1,0:T(8,128)(2,1)S(1)} %ssd.1) | data formatting | bytes 5242880
Async XLA Ops:
  1.1 1.7 %copy-start = (bf16[2048,640]{1,0:T(8,128)(2,1)S(1)}, bf16[2048,640]{1,0:T(8,128)(2,1)}, u32[]{:S(2)}) copy-start(bf16[2048,640]{1,0:T(8,128)(2,1)} %x_hbm.1) | copy-start | bytes 7864324
  2.9 0.8 %copy-start.1 = (bf16[256,128]{1,0:T(8,128)(2,1)S(1)}, bf16[256,128]{1,0:T(8,128)(2,1)}, u32[]{:S(2)}) copy-start(bf16[256,128]{1,0:T(8,128)(2,1)} %b_hbm.1) | copy-start | bytes 196612
  3.7 0.8 %copy-start.2 = (bf16[256,128]{1,0:T(8,128)(2,1)S(1)}, bf16[256,128]{1,0:T(8,128)(2,1)}, u32[]{:S(2)}) copy-start(bf16[256,128]{1,0:T(8,128)(2,1)} %c_hbm.1) | copy-start | bytes 196612
  4.6 0.7 %copy-start.3 = (f32[5120]{0:T(1024)S(1)}, f32[5120]{0:T(1024)}, u32[]{:S(2)}) copy-start(f32[5120]{0:T(1024)} %param.15) | copy-start | bytes 61444
  5.3 0.7 %copy-start.4 = (f32[80]{0:T(128)S(1)}, f32[80]{0:T(128)}, u32[]{:S(2)}) copy-start(f32[80]{0:T(128)} %decay_ref.1) | copy-start | bytes 964
  5.9 0.7 %copy-start.5 = (f32[80]{0:T(128)S(1)}, f32[80]{0:T(128)}, u32[]{:S(2)}) copy-start(f32[80]{0:T(128)} %skip_ref.1) | copy-start | bytes 964
